TPU v7x, 128 devices: a whole 4x4x4 slice. The times are simulated.
128 devices in a mesh: dp: 8 (over z, core), mp: 16 (over x, y).
Axes of the slice: x: 4, y: 4, z: 4, core: 2. Of those that a mesh axis runs over, the one named last changes fastest.
Arguments:
- features: bfloat16 [8192, 2048], P('dp'), may hold values from -21 to 21
- rewards: float32 [32, 256], P('dp'), may hold values from -6 to 6
- old_values: float32 [32, 256], P('dp'), may hold values from -6 to 6
- dones: int32 [32, 256], P('dp'), may hold values 0 or 1
- lengths: int32 [32], P('dp'), may hold values from 128 to 256
- proj_weights: bfloat16 [2048, 2, 8192], P(None, None, 'mp'), may hold values from -0.125 to 0.125
- down_weight: bfloat16 [8192, 2048], P('mp'), may hold values from -0.0625 to 0.0625
- value_head: float32 [2048], replicated, may hold values from -0.0078125 to 0.0078125
- master: float32 [2048, 2, 8192], P('dp', None, 'mp'), may hold values from -0.125 to 0.125
- moment: float32 [2048, 2, 8192], P('dp', None, 'mp'), may hold values from -1.035801e-05 to 1.035801e-05
- second: float32 [2048, 2, 8192], P('dp', None, 'mp'), may hold values from 2.9802322e-13 to 2.9802322e-12
Outputs:
- master_new: float32 [2048, 2, 8192], P('dp', None, 'mp')
- moment_new: float32 [2048, 2, 8192], P('dp', None, 'mp')
- second_new: float32 [2048, 2, 8192], P('dp', None, 'mp')
- working: bfloat16 [2048, 2, 8192], P(None, None, 'mp')
- total_loss: float32 [], replicated
All inputs are finite; a program needn't handle non-finite values. No bound on the sum of `dones` on one device may be relied on, other than what follows from the above.
Results may differ from a plain program's by a relative error of at most 0.0011.
Values may be sent and summed in bfloat16 or wider, within the bound.
A program may use at most 128 MiB of HBM per device.

v0:
```python
import functools
import math
import jax
import jax.numpy as jnp
from jax import lax
from jax.sharding import Mesh
from jax.sharding import PartitionSpec as P

DP = ("dp_0", "dp_1")
MP = ("mp_0", "mp_1")
DP_MP = ("dp_0", "dp_1", "mp_0", "mp_1")
GAMMA = 0.99
LAMBDA = 0.95
MAX_NORM = 0.05


def own_block(parts, axes, sequence):
    shape = [lax.axis_size(a) for a in axes]
    parts = parts.reshape(*shape, *parts.shape[1:])
    parts = parts.transpose(*sequence, *range(len(axes), parts.ndim))
    parts = parts.reshape(-1, *parts.shape[len(axes) :])
    for k in sequence:
        parts = lax.psum_scatter(parts, axes[k], scatter_dimension=0, tiled=True)
    return parts[0]


def in_blocks(value, dim, count):
    before, after = (value.shape[:dim], value.shape[dim + 1 :])
    return jnp.moveaxis(value.reshape(*before, count, -1, *after), dim, 0)


def summed_rows(value, axes, sequence, dim):
    count = lax.axis_size(axes)
    return own_block(in_blocks(value, dim, count), axes, sequence)


def one_axis_at_a_time(value, axes):
    return functools.reduce(lax.psum, axes, value)


def gae_targets(rewards, old_values, dones, lengths):
    seq_len = rewards.shape[1]
    keeps = 1.0 - dones.astype(jnp.float32)
    following = jnp.concatenate([old_values[:, 1:], jnp.zeros_like(old_values[:, :1])], axis=1)
    deltas = rewards + GAMMA * following * keeps - old_values
    counted = jnp.cumsum(dones, axis=1) - dones
    places = jnp.arange(seq_len, dtype=jnp.int32)
    spans = places[None, :] - places[:, None]
    linked = (counted[:, :, None] == counted[:, None, :]) & (spans[None] >= 0)
    powers = jnp.exp(jnp.maximum(spans, 0).astype(jnp.float32) * math.log(GAMMA * LAMBDA))
    kernel = jnp.where(linked, powers[None], jnp.zeros((), jnp.float32))
    advantage = jnp.einsum("ats,as->at", kernel, deltas, precision=lax.Precision.HIGHEST)
    targets = (advantage + old_values).reshape(-1)
    mask = (places[None, :] < lengths[:, None]).astype(jnp.float32).reshape(-1)
    return (targets, mask)


def value_loss(features, mixed, targets, mask, value_head, total_tokens):
    stream = features.astype(jnp.float32) + mixed
    norm_factor = lax.rsqrt(jnp.mean(stream * stream, axis=-1) + 1e-05)
    normed = stream * norm_factor[:, None]
    estimate = jnp.dot(normed, value_head, precision=lax.Precision.HIGHEST)
    errors = estimate - targets
    loss_part = jnp.sum(mask * errors * errors) / total_tokens
    coeff = 2.0 * mask * errors / total_tokens
    head_grad = coeff[:, None] * value_head[None, :]
    out_grad = (
        norm_factor[:, None]
        * (head_grad - normed * jnp.mean(head_grad * normed, axis=-1, keepdims=True))
    ).astype(jnp.bfloat16)
    return (loss_part, out_grad)


def contract_rows(left, right):
    return lax.dot_general(
        left, right, (((0,), (0,)), ((), ())), preferred_element_type=jnp.float32
    )


def per_device(
    features,
    rewards,
    old_values,
    dones,
    lengths,
    proj_weights,
    down_weight,
    value_head,
    master,
    moment,
    second,
):
    token_count = features.shape[0]
    model_width = features.shape[1]
    ff_local = down_weight.shape[0]
    data_ways = lax.axis_size(DP)
    model_ways = lax.axis_size(MP)
    total_tokens = token_count * data_ways
    targets, mask = gae_targets(rewards, old_values, dones, lengths)
    both = jnp.dot(
        features,
        proj_weights.reshape(model_width, 2 * ff_local),
        preferred_element_type=jnp.float32,
    )
    both = both.reshape(token_count, 2, ff_local)
    gate_values = both[:, 0, :]
    up_values = both[:, 1, :]
    hidden = (jax.nn.silu(gate_values) * up_values).astype(jnp.bfloat16)
    mixed = lax.psum(
        jnp.dot(hidden, down_weight, preferred_element_type=jnp.float32).astype(jnp.bfloat16), MP
    ).astype(jnp.float32)
    loss_part, out_grad = value_loss(features, mixed, targets, mask, value_head, total_tokens)
    loss_part = loss_part / model_ways
    hidden_grad = jnp.dot(out_grad, down_weight.T, preferred_element_type=jnp.float32)
    gate_sigmoid = jax.nn.sigmoid(gate_values)
    gate_grad = (
        hidden_grad * up_values * gate_sigmoid * (1.0 + gate_values * (1.0 - gate_sigmoid))
    ).astype(jnp.bfloat16)
    up_grad = (hidden_grad * gate_values * gate_sigmoid).astype(jnp.bfloat16)
    both_grad = jnp.stack([gate_grad, up_grad], axis=1).reshape(token_count, 2 * ff_local)
    row_share = model_width // data_ways
    grads = summed_rows(
        contract_rows(features, both_grad).reshape(row_share * lax.axis_size(DP), 2, ff_local),
        DP,
        (1, 0),
        0,
    )
    squares = jnp.sum(grads * grads)
    squared_total, total_loss = (
        one_axis_at_a_time(squares, DP_MP),
        one_axis_at_a_time(loss_part, DP_MP),
    )
    clip = jnp.minimum(1.0, MAX_NORM / (jnp.sqrt(squared_total) + 1e-06))
    clipped = clip * grads
    moment_new = 0.9 * moment + 0.1 * clipped
    second_new = 0.999 * second + 0.001 * clipped * clipped
    first_hat = moment_new / (1.0 - 0.9**10)
    second_hat = second_new / (1.0 - 0.999**10)
    master_new = master - 0.001 * (first_hat / (jnp.sqrt(second_hat) + 1e-08) + 0.1 * master)
    working = lax.all_gather(master_new.astype(jnp.bfloat16), DP, axis=0, tiled=True)
    return (master_new, moment_new, second_new, working, total_loss)


def solution(mesh):
    finer = Mesh(mesh.devices.reshape(4, 2, 4, 4), ("dp_0", "dp_1", "mp_0", "mp_1"))
    return jax.shard_map(
        per_device,
        mesh=finer,
        in_specs=(
            P(DP, None),
            P(DP, None),
            P(DP, None),
            P(DP, None),
            P(DP),
            P(None, None, MP),
            P(MP, None),
            P(),
            P(DP, None, MP),
            P(DP, None, MP),
            P(DP, None, MP),
        ),
        out_specs=(P(DP, None, MP), P(DP, None, MP), P(DP, None, MP), P(None, None, MP), P()),
        check_vma=False,
    )
```

profile of v0, /device:TPU:1, one launch (start us, length us, event | category | flops | bytes accessed | tf_op | source)
XLA Modules:
  0.0 348.5 jit_solution(17223176488133655442)
XLA Ops:
  7.2 0.0 copy-start
  7.2 0.0 all-reduce.7.cloned.1.call-start
  7.2 5.5 %copy.34 = bf16[256,8,2,512]{3,1,2,0:T(8,128)(2,1)} copy(bf16[256,8,2,512]{3,2,1,0:T(2,128)(2,1)} %bitcast.73) | data formatting | bytes 8388608
  12.8 6.5 %copy.21 = bf16[1024,2048]{1,0:T(8,128)(2,1)} copy(bf16[1024,2048]{0,1:T(8,128)(2,1)} %bitcast.72) | data formatting | bytes 8388608 | tf_op jit(solution)/shard_map/dot_general | solution.py:100
  19.3 7.6 %fusion.6 = f32[1024,2,512]{0,2,1:T(8,128)S(1)} fusion(bf16[2,512,2048]{2,1,0:T(8,128)(2,1)} %bitcast.74, bf16[1024,2048]{1,0:T(8,128)(2,1)} %param.11), kind=kOutput, calls=%fused_computation.10 | convolution fusion | flops 4294967296 | bytes 12582912 | tf_op jit(solution)/shard_map/dot_general | solution.py:100
  26.9 0.0 copy-start.9
  26.9 2.0 copy-done.9
  28.9 0.0 copy-done
  28.9 4.4 %convolution_convert_fusion = bf16[1024,2048]{1,0:T(8,128)(2,1)} fusion(bf16[512,2048]{1,0:T(8,128)(2,1)S(1)} %copy-done, f32[1024,2,512]{0,2,1:T(8,128)S(1)} %fusion.6), kind=kOutput, calls=%fused_computation.14 | convolution fusion | flops 2152726528 | bytes 10485760 | tf_op jit(solution)/shard_map/dot_general | solution.py:110
  33.3 0.0 copy-start.8
  33.3 0.0 copy-start.5
  33.3 0.0 copy-start.4
  33.3 0.0 all-reduce.7.cloned.1.call-update
  33.4 0.2 reduce-scatter.3.cloned.1.call-start
  33.6 0.4 copy-done.8
  34.0 0.1 iota_compare_fusion
  34.1 0.0 copy-done.5
  34.1 0.1 slice.19
  34.1 0.0 copy-done.4
  34.2 1.2 reduce-window.6
  35.4 0.1 slice.22
  35.4 0.1 copy.22
  35.6 0.1 copy.23
  35.7 0.1 multiply_exponential_fusion
  35.8 0.1 add_bitcast_fusion
  35.9 0.0 copy-done.7
  35.9 1.2 fusion.13
  37.1 0.0 copy-start.6
  37.1 102.5 %all-reduce.7.cloned.1.call-done = bf16[1024,2048]{1,0:T(8,128)(2,1)} async-done(((bf16[1024,2048]{1,0:T(8,128)(2,1)}), bf16[1024,2048]{1,0:T(8,128)(2,1)}) %all-reduce.7.cloned.1.call-update) | async-done | bytes 4194320 | tf_op jit(solution)/shard_map/psum | solution.py:109
  139.7 0.0 copy-start.2
  139.7 0.0 copy-start.3
  139.7 5.0 %multiply_reduce_fusion = f32[1024]{0:T(1024)S(1)} fusion(bf16[1024,2048]{1,0:T(8,128)(2,1)} %all-reduce.7.cloned.1.call-done, bf16[1024,2048]{1,0:T(8,128)(2,1)} %param.11), kind=kLoop, calls=%fused_computation.5 | loop fusion | flops 10484736 | bytes 8392704 | tf_op jit(solution)/shard_map/reduce_sum | solution.py:60
  144.7 0.0 copy-done.6
  144.7 0.0 copy-done.2
  144.7 0.9 copy-done.3
  145.6 8.1 %fusion.4 = f32[1,1024]{1,0:T(1,128)S(1)} fusion(f32[2048,1]{0,1:T(1,128)S(1)} %bitcast.76, bf16[1024,2048]{1,0:T(8,128)(2,1)S(1)} %copy-done.3, bf16[1024,2048]{1,0:T(8,128)(2,1)S(1)} %copy-done.2, f32[1024]{0:T(1024)S(1)} %add_rsqrt_fusion), kind=kOutput, calls=%fused_computation.8 | convolution fusion | flops 33554432 | bytes 8404992 | tf_op jit(solution)/shard_map/dot_general | solution.py:62
  153.7 0.6 fusion.26
  154.4 2.6 fusion
  156.9 0.0 copy-done.10
  156.9 5.4 %fusion.19 = (bf16[1024,1,512]{0,2,1:T(8,128)(2,1)S(1)}, bf16[1024,1,512]{0,2,1:T(8,128)(2,1)S(1)}) fusion(f32[1024,2,512]{0,2,1:T(8,128)S(1)} %copy-done.10, bf16[512,2048]{1,0:T(8,128)(2,1)S(1)} %copy-done, bf16[1024,2048]{1,0:T(8,128)(2,1)S(1)} %copy-done.3, bf16[1024,2048]{1,0:T(8,128)(2,1)S(1)} %copy-done.2, f32[1024]{0:T(1024)S(1)} %broadcast_multiply_fusion, ...), kind=kOutput, calls=%fused_computation.36 | convolution fusion | flops 2173173760 | bytes 16797696 | tf_op jit(solution)/shard_map/dot_general | solution.py:114
  162.4 0.2 pad_maximum_fusion
  162.6 6.7 %convolution_bitcast_fusion = f32[2048,1024]{0,1:T(8,128)} fusion(bf16[1024,1024]{0,1:T(8,128)(2,1)S(1)} %bitcast.75, bf16[1024,2048]{1,0:T(8,128)(2,1)S(1)} %copy-done.2), kind=kOutput, calls=%fused_computation.9 | convolution fusion | flops 4294967296 | bytes 14680064 | tf_op jit(solution)/shard_map/dot_general | solution.py:75
  169.3 11.7 %reshape_reshape_reshape.3 = f32[4,2,256,2,512]{2,1,0,4,3:T(2,128)} reshape(f32[2048,1024]{0,1:T(8,128)} %convolution_bitcast_fusion) | data formatting | bytes 16777216 | tf_op jit(solution)/shard_map/reshape;reshape;reshape | solution.py:19
  181.0 13.1 %copy.24 = f32[2,4,256,2,512]{4,2,3,1,0:T(8,128)} copy(f32[2,4,256,2,512]{2,0,1,4,3:T(2,128)} %bitcast.71) | data formatting | bytes 16777216 | tf_op jit(solution)/shard_map/transpose | solution.py:20
  194.1 0.0 reduce-scatter.3.cloned.1.call-update
  194.1 0.0 reduce-scatter.5.cloned.1.call-start
  194.2 19.7 %reduce-scatter.3.cloned.1.call-done = f32[4,256,2,512]{3,1,2,0:T(8,128)} async-done(((f32[8,256,2,512]{3,1,2,0:T(8,128)}), f32[4,256,2,512]{3,1,2,0:T(8,128)}) %reduce-scatter.3.cloned.1.call-update) | async-done | bytes 4194320 | tf_op jit(solution)/shard_map/reduce_scatter | solution.py:23
  213.9 0.0 reduce-scatter.5.cloned.1.call-update
  213.9 0.0 all-gather.2.cloned.1.call-start
  214.6 49.8 %reduce-scatter.5.cloned.1.call-done = f32[1,256,2,512]{3,1,2,0:T(8,128)} async-done(((f32[4,256,2,512]{3,1,2,0:T(8,128)}), f32[1,256,2,512]{3,1,2,0:T(8,128)}) %reduce-scatter.5.cloned.1.call-update) | async-done | bytes 1048592 | tf_op jit(solution)/shard_map/reduce_scatter | solution.py:23
  264.4 2.1 multiply_reduce_fusion.1
  266.5 7.1 %all-reduce.3 = (f32[]{:T(128)}, f32[]{:T(128)}) all-reduce(f32[]{:T(128)} %multiply_reduce_fusion.1, f32[]{:T(128)S(6)} %div.55), channel_id=1, replica_groups=mesh['dp_0'=4,'dp_1'=2,'mp_0'=4,'mp_1'=4] {'dp_0'}, use_global_device_ids=true, to_apply=%region_8.9 | all-reduce | flops 2 | bytes 16 | tf_op jit(solution)/shard_map/psum | solution.py:38
  273.6 5.5 %all-reduce.4 = (f32[]{:T(128)}, f32[]{:T(128)}) all-reduce(f32[]{:T(128)} %get-tuple-element.14, f32[]{:T(128)} %get-tuple-element.15), channel_id=1, replica_groups=mesh['dp_0'=4,'dp_1'=2,'mp_0'=4,'mp_1'=4] {'dp_1'}, use_global_device_ids=true, to_apply=%region_9.10 | all-reduce | flops 2 | bytes 16 | tf_op jit(solution)/shard_map/psum | solution.py:38
  279.1 9.0 %all-reduce.2 = (f32[]{:T(128)}, f32[]{:T(128)}) all-reduce(f32[]{:T(128)} %get-tuple-element.16, f32[]{:T(128)} %get-tuple-element.17), channel_id=1, replica_groups=mesh['dp_0'=4,'dp_1'=2,'mp_0'=4,'mp_1'=4] {'mp_0'}, use_global_device_ids=true, to_apply=%region_10.11 | all-reduce | flops 2 | bytes 16 | tf_op jit(solution)/shard_map/psum | solution.py:38
  288.1 9.1 %all-reduce.1 = (f32[]{:T(128)}, f32[]{:T(128)}) all-reduce(f32[]{:T(128)} %get-tuple-element.12, f32[]{:T(128)} %get-tuple-element.13), channel_id=1, replica_groups=mesh['dp_0'=4,'dp_1'=2,'mp_0'=4,'mp_1'=4] {'mp_1'}, use_global_device_ids=true, to_apply=%region_11.12 | all-reduce | flops 2 | bytes 16 | tf_op jit(solution)/shard_map/psum | solution.py:38
  297.9 3.2 fusion.31
  301.1 1.3 copy.28
  302.4 0.0 all-gather.2.cloned.1.call-update
  302.5 1.8 copy.29
  304.2 1.8 copy.30
  306.0 1.8 copy.31
  307.8 26.3 %all-gather.2.cloned.1.call-done = bf16[2048,2,512]{2,1,0:T(2,128)(2,1)} async-done(((bf16[256,2,512]{2,1,0:T(2,128)(2,1)}), bf16[2048,2,512]{2,1,0:T(2,128)(2,1)}) %all-gather.2.cloned.1.call-update) | async-done | bytes 4194320 | tf_op jit(solution)/shard_map/all_gather | solution.py:140
  334.1 7.8 %copy.53 = bf16[2048,2,512]{2,1,0:T(2,128)(2,1)} copy(bf16[2048,2,512]{2,1,0:T(2,128)(2,1)} %all-gather.2.cloned.1.call-done) | data formatting | bytes 8388608
  341.9 0.0 copy-done.1
  (14 shorter events, 0.2 us)
Async XLA Ops:
  7.2 21.7 %copy-start = (bf16[512,2048]{1,0:T(8,128)(2,1)S(1)}, bf16[512,2048]{1,0:T(8,128)(2,1)}, u32[]{:S(2)}) copy-start(bf16[512,2048]{1,0:T(8,128)(2,1)} %param.17) | copy-start | bytes 6291460
  7.2 132.5 %all-reduce.7.cloned.1.call-start = ((), (), s32[]{:S(2)}) async-start(), calls=%async_computation.2 | async-start | bytes 8388608 | tf_op jit(solution)/shard_map/psum | solution.py:109
  26.9 2.0 copy-start.9
  33.3 0.7 copy-start.8
  33.3 0.7 copy-start.5
  33.3 0.8 copy-start.4
  33.3 2.5 copy-start.7
  33.4 180.5 %reduce-scatter.3.cloned.1.call-start = ((), (), s32[]{:S(2)}) async-start(), calls=%async_computation.3 | async-start | bytes 12582912 | tf_op jit(solution)/shard_map/reduce_scatter | solution.py:23
  37.1 107.6 %copy-start.6 = (f32[2048]{0:T(1024)S(1)}, f32[2048]{0:T(1024)}, u32[]{:S(2)}) copy-start(f32[2048]{0:T(1024)} %param.18) | copy-start | bytes 24580
  139.7 5.1 %copy-start.2 = (bf16[1024,2048]{1,0:T(8,128)(2,1)S(1)}, bf16[1024,2048]{1,0:T(8,128)(2,1)}, u32[]{:S(2)}) copy-start(bf16[1024,2048]{1,0:T(8,128)(2,1)} %param.11) | copy-start | bytes 12582916
  139.7 5.9 %copy-start.3 = (bf16[1024,2048]{1,0:T(8,128)(2,1)S(1)}, bf16[1024,2048]{1,0:T(8,128)(2,1)}, u32[]{:S(2)}) copy-start(bf16[1024,2048]{1,0:T(8,128)(2,1)} %all-reduce.7.cloned.1.call-done) | copy-start | bytes 12582916
  154.3 2.6 copy-start.10
  194.1 70.3 %reduce-scatter.5.cloned.1.call-start = ((), (), s32[]{:S(2)}) async-start(), calls=%async_computation.4 | async-start | bytes 5242880 | tf_op jit(solution)/shard_map/reduce_scatter | solution.py:23
  213.9 120.2 %all-gather.2.cloned.1.call-start = ((), (), s32[]{:S(2)}) async-start(), calls=%async_computation.5 | async-start | bytes 4718592 | tf_op jit(solution)/shard_map/all_gather | solution.py:140
  334.1 7.9 %copy-start.1 = (bf16[512,2048]{1,0:T(8,128)(2,1)S(1)}, bf16[512,2048]{1,0:T(8,128)(2,1)}, u32[]{:S(2)}) copy-start(bf16[512,2048]{1,0:T(8,128)(2,1)} %param.17) | copy-start | bytes 6291460
Sparse Core Ops, SparseCore 0:
  33.5 106.1 all-reduce.6
  194.2 19.5 reduce-scatter.2
  216.3 48.0 reduce-scatter.4
  302.6 31.4 all-gather.1
where the time goes:
time: 350 us; the launch traced here: 348 us
  waiting for transfers between devices  198 us (57%)
  local copies, waits for them, and re-layouts  55.1 us (16%)
  matrix products  33.5 us (10%)
  blocking collectives  30.7 us (9%)
  other arithmetic  15.3 us (4%)
  between operations  15.3 us (4%)
    psum x1, waiting for transfers between devices, per_device(): lax.psum(jnp.dot(hidden, down_weight, preferred_element_type=jnp.float32)...  103 us
    reduce_scatter x2, waiting for transfers between devices, own_block(): parts = lax.psum_scatter(parts, axes[k], scatter_dimension=0, tiled=True)  69.5 us
    psum x4, blocking collectives, one_axis_at_a_time(): return functools.reduce(lax.psum, axes, value)  30.7 us
    all_gather x1, waiting for transfers between devices, per_device(): lax.all_gather(master_new.astype(jnp.bfloat16), DP, axis=0, tiled=True)  26.3 us
    unnamed x28, local copies, waits for them, and re-layouts  22 us
    transpose x1, local copies, waits for them, and re-layouts, own_block(): parts = parts.transpose(*sequence, *range(len(axes), parts.ndim))  13.1 us
    another operation x1, local copies, waits for them, and re-layouts, own_block(): parts = parts.reshape(*shape, *parts.shape[1:])  11.7 us
    dot_general x1, matrix products, value_loss(): estimate = jnp.dot(normed, value_head, precision=lax.Precision.HIGHEST)  8.13 us
  transfers between devices with their start and end apart: 4, of which 4 were waited for; matrix products, arithmetic and copies ran while one was open for 2% of the time, Pallas kernels for 0%

commit v1 on v0

--- a/solution.py
+++ b/solution.py
@@ -106,8 +106,12 @@
     gate_values = both[:, 0, :]
     up_values = both[:, 1, :]
     hidden = (jax.nn.silu(gate_values) * up_values).astype(jnp.bfloat16)
-    mixed = lax.psum(
-        jnp.dot(hidden, down_weight, preferred_element_type=jnp.float32).astype(jnp.bfloat16), MP
+    mixed = jnp.sum(
+        lax.all_gather(
+            jnp.dot(hidden, down_weight, preferred_element_type=jnp.float32).astype(jnp.bfloat16),
+            MP,
+        ),
+        axis=0,
     ).astype(jnp.float32)
     loss_part, out_grad = value_loss(features, mixed, targets, mask, value_head, total_tokens)
     loss_part = loss_part / model_ways

time: 350 us -> 638 us (1.82)
  waiting for transfers between devices: 198 us -> 463 us
  other arithmetic: 15.3 us -> 39 us
    all_gather x0 -> x1, waiting for transfers between devices: none -> 368 us  [per_device(): lax.all_gather(jnp.dot(hidden, down_weight, preferred_element_type=jnp.fl...]
    psum x1 -> x0, waiting for transfers between devices: 103 us -> none  [per_device(): lax.psum(jnp.dot(hidden, down_weight, preferred_element_type=jnp.float32)...]
    reduce_sum x0 -> x1, other arithmetic: none -> 23.7 us  [per_device(): jnp.sum(lax.all_gather(jnp.dot(hidden, down_weight, preferred_element_typ...]
  transfers between devices with their start and end apart: 4 -> 4, of which waited for: 4 -> 4; matrix products, arithmetic and copies ran while one was open for 2% -> 1% of each run, Pallas kernels for 0% -> 0%
where the time goes in v1:
time: 638 us; the launch traced here: 637 us
  waiting for transfers between devices  463 us (73%)
  local copies, waits for them, and re-layouts  55.1 us (9%)
  other arithmetic  39 us (6%)
  matrix products  33.2 us (5%)
  blocking collectives  30.7 us (5%)
  between operations  15.3 us (2%)
    all_gather x1, waiting for transfers between devices, per_device(): lax.all_gather(jnp.dot(hidden, down_weight, preferred_element_type=jnp.fl...  368 us
    reduce_scatter x2, waiting for transfers between devices, own_block(): parts = lax.psum_scatter(parts, axes[k], scatter_dimension=0, tiled=True)  69.2 us
    psum x4, blocking collectives, one_axis_at_a_time(): return functools.reduce(lax.psum, axes, value)  30.7 us
    all_gather x1, waiting for transfers between devices, per_device(): lax.all_gather(master_new.astype(jnp.bfloat16), DP, axis=0, tiled=True)  26.3 us
    reduce_sum x1, other arithmetic, per_device(): jnp.sum(lax.all_gather(jnp.dot(hidden, down_weight, preferred_element_typ...  23.7 us
    unnamed x28, local copies, waits for them, and re-layouts  22.1 us
    transpose x1, local copies, waits for them, and re-layouts, own_block(): parts = parts.transpose(*sequence, *range(len(axes), parts.ndim))  13.1 us
  transfers between devices with their start and end apart: 4, of which 4 were waited for; matrix products, arithmetic and copies ran while one was open for 1% of the time, Pallas kernels for 0%

profile of v1, /device:TPU:1, one launch (start us, length us, event | category | flops | bytes accessed | tf_op | source)
XLA Modules:
  0.0 637.0 jit_solution(14763888266237457050)
XLA Ops:
  7.2 0.0 copy-start
  7.2 0.0 all-gather.6.cloned.1.call-start
  7.2 5.5 copy.34
  12.8 6.5 %copy.21 = bf16[1024,2048]{1,0:T(8,128)(2,1)} copy(bf16[1024,2048]{0,1:T(8,128)(2,1)} %bitcast.73) | data formatting | bytes 8388608 | tf_op jit(solution)/shard_map/dot_general | solution.py:100
  19.3 7.6 %fusion.6 = f32[1024,2,512]{0,2,1:T(8,128)S(1)} fusion(bf16[2,512,2048]{2,1,0:T(8,128)(2,1)} %bitcast.75, bf16[1024,2048]{1,0:T(8,128)(2,1)} %param.11), kind=kOutput, calls=%fused_computation.10 | convolution fusion | flops 4294967296 | bytes 12582912 | tf_op jit(solution)/shard_map/dot_general | solution.py:100
  26.9 0.0 copy-start.9
  26.9 2.0 copy-done.9
  28.9 0.0 copy-done
  28.9 4.4 convolution_convert_fusion
  33.3 0.0 copy-start.4
  33.3 0.0 copy-start.5
  33.3 0.0 copy-start.7
  33.3 0.0 copy-start.8
  33.3 0.0 all-gather.6.cloned.1.call-update
  33.4 0.2 reduce-scatter.3.cloned.1.call-start
  33.6 0.4 copy-done.4
  34.0 1.2 reduce-window.6
  35.2 0.1 slice.22
  35.3 0.1 copy.22
  35.4 0.1 copy.23
  35.5 0.0 copy-done.5
  35.5 0.1 slice.19
  35.7 0.1 multiply_exponential_fusion
  35.7 0.1 add_bitcast_fusion
  35.8 0.0 copy-done.7
  35.8 1.2 fusion.13
  37.1 0.0 copy-done.8
  37.1 0.1 iota_compare_fusion
  37.2 367.8 %all-gather.6.cloned.1.call-done = bf16[16384,2048]{1,0:T(8,128)(2,1)} async-done(((bf16[1024,2048]{1,0:T(8,128)(2,1)}), bf16[16384,2048]{1,0:T(8,128)(2,1)}) %all-gather.6.cloned.1.call-update) | async-done | bytes 67108880 | tf_op jit(solution)/shard_map/all_gather | solution.py:110
  404.9 23.7 %reduce_sum.48 = bf16[1024,2048]{1,0:T(8,128)(2,1)} reduce(bf16[16,1024,2048]{2,1,0:T(8,128)(2,1)} %bitcast.5, bf16[]{:T(256)} %constant.23.clone.1), dimensions={0}, to_apply=%region_0.0 | reduce | flops 31457280 | bytes 71303168 | tf_op jit(solution)/shard_map/reduce_sum | solution.py:109
  428.7 0.0 copy-start.2
  428.7 5.0 multiply_reduce_fusion
  433.7 0.0 copy-done.2
  433.7 0.9 copy-done.3
  434.6 0.0 copy-done.6
  434.6 8.1 %fusion.4 = f32[1,1024]{1,0:T(1,128)S(1)} fusion(f32[2048,1]{0,1:T(1,128)S(1)} %bitcast.77, bf16[1024,2048]{1,0:T(8,128)(2,1)S(1)} %copy-done.2, bf16[1024,2048]{1,0:T(8,128)(2,1)S(1)} %copy-done.3, f32[1024]{0:T(1024)S(1)} %add_rsqrt_fusion), kind=kOutput, calls=%fused_computation.8 | convolution fusion | flops 33554432 | bytes 8404992 | tf_op jit(solution)/shard_map/dot_general | solution.py:62
  442.7 0.6 fusion.26
  443.4 2.5 fusion
  445.9 0.0 copy-done.10
  445.9 5.2 fusion.19
  451.1 0.2 pad_maximum_fusion
  451.3 6.7 %convolution_bitcast_fusion = f32[2048,1024]{0,1:T(8,128)} fusion(bf16[1024,1024]{0,1:T(8,128)(2,1)S(1)} %bitcast.76, bf16[1024,2048]{1,0:T(8,128)(2,1)S(1)} %copy-done.3), kind=kOutput, calls=%fused_computation.9 | convolution fusion | flops 4294967296 | bytes 14680064 | tf_op jit(solution)/shard_map/dot_general | solution.py:75
  458.0 11.7 %reshape_reshape_reshape.3 = f32[4,2,256,2,512]{2,1,0,4,3:T(2,128)} reshape(f32[2048,1024]{0,1:T(8,128)} %convolution_bitcast_fusion) | data formatting | bytes 16777216 | tf_op jit(solution)/shard_map/reshape;reshape;reshape | solution.py:19
  469.7 13.1 %copy.24 = f32[2,4,256,2,512]{4,2,3,1,0:T(8,128)} copy(f32[2,4,256,2,512]{2,0,1,4,3:T(2,128)} %bitcast.72) | data formatting | bytes 16777216 | tf_op jit(solution)/shard_map/transpose | solution.py:20
  482.8 0.0 reduce-scatter.3.cloned.1.call-update
  482.8 0.0 reduce-scatter.5.cloned.1.call-start
  482.9 19.5 %reduce-scatter.3.cloned.1.call-done = f32[4,256,2,512]{3,1,2,0:T(8,128)} async-done(((f32[8,256,2,512]{3,1,2,0:T(8,128)}), f32[4,256,2,512]{3,1,2,0:T(8,128)}) %reduce-scatter.3.cloned.1.call-update) | async-done | bytes 4194320 | tf_op jit(solution)/shard_map/reduce_scatter | solution.py:23
  502.4 0.0 reduce-scatter.5.cloned.1.call-update
  502.4 0.0 all-gather.4.cloned.1.call-start
  503.1 49.8 %reduce-scatter.5.cloned.1.call-done = f32[1,256,2,512]{3,1,2,0:T(8,128)} async-done(((f32[4,256,2,512]{3,1,2,0:T(8,128)}), f32[1,256,2,512]{3,1,2,0:T(8,128)}) %reduce-scatter.5.cloned.1.call-update) | async-done | bytes 1048592 | tf_op jit(solution)/shard_map/reduce_scatter | solution.py:23
  552.9 2.1 multiply_reduce_fusion.1
  555.0 7.1 %all-reduce.3 = (f32[]{:T(128)}, f32[]{:T(128)}) all-reduce(f32[]{:T(128)} %multiply_reduce_fusion.1, f32[]{:T(128)S(6)} %div.55), channel_id=1, replica_groups=mesh['dp_0'=4,'dp_1'=2,'mp_0'=4,'mp_1'=4] {'dp_0'}, use_global_device_ids=true, to_apply=%region_8.9 | all-reduce | flops 2 | bytes 16 | tf_op jit(solution)/shard_map/psum | solution.py:38
  562.1 5.5 all-reduce.4
  567.6 9.0 %all-reduce.2 = (f32[]{:T(128)}, f32[]{:T(128)}) all-reduce(f32[]{:T(128)} %get-tuple-element.16, f32[]{:T(128)} %get-tuple-element.17), channel_id=1, replica_groups=mesh['dp_0'=4,'dp_1'=2,'mp_0'=4,'mp_1'=4] {'mp_0'}, use_global_device_ids=true, to_apply=%region_10.11 | all-reduce | flops 2 | bytes 16 | tf_op jit(solution)/shard_map/psum | solution.py:38
  576.6 9.1 %all-reduce.1 = (f32[]{:T(128)}, f32[]{:T(128)}) all-reduce(f32[]{:T(128)} %get-tuple-element.12, f32[]{:T(128)} %get-tuple-element.13), channel_id=1, replica_groups=mesh['dp_0'=4,'dp_1'=2,'mp_0'=4,'mp_1'=4] {'mp_1'}, use_global_device_ids=true, to_apply=%region_11.12 | all-reduce | flops 2 | bytes 16 | tf_op jit(solution)/shard_map/psum | solution.py:38
  586.4 3.2 fusion.31
  589.6 1.3 copy.28
  590.9 0.0 all-gather.4.cloned.1.call-update
  590.9 1.8 copy.29
  592.7 1.8 copy.30
  594.5 1.8 copy.31
  596.3 26.3 %all-gather.4.cloned.1.call-done = bf16[2048,2,512]{2,1,0:T(2,128)(2,1)} async-done(((bf16[256,2,512]{2,1,0:T(2,128)(2,1)}), bf16[2048,2,512]{2,1,0:T(2,128)(2,1)}) %all-gather.4.cloned.1.call-update) | async-done | bytes 4194320 | tf_op jit(solution)/shard_map/all_gather | solution.py:144
  622.6 7.8 %copy.52 = bf16[2048,2,512]{2,1,0:T(2,128)(2,1)} copy(bf16[2048,2,512]{2,1,0:T(2,128)(2,1)} %all-gather.4.cloned.1.call-done) | data formatting | bytes 8388608
  630.4 0.0 copy-done.1
  (15 shorter events, 0.2 us)
Async XLA Ops:
  7.2 21.7 %copy-start = (bf16[512,2048]{1,0:T(8,128)(2,1)S(1)}, bf16[512,2048]{1,0:T(8,128)(2,1)}, u32[]{:S(2)}) copy-start(bf16[512,2048]{1,0:T(8,128)(2,1)} %param.17) | copy-start | bytes 6291460
  7.2 397.7 %all-gather.6.cloned.1.call-start = ((), (), s32[]{:S(2)}) async-start(), calls=%async_computation.5 | async-start | bytes 71303168 | tf_op jit(solution)/shard_map/all_gather | solution.py:110
  26.9 2.0 copy-start.9
  33.3 0.7 copy-start.4
  33.3 2.2 copy-start.5
  33.3 2.5 copy-start.7
  33.3 3.7 copy-start.8
  33.4 469.0 %reduce-scatter.3.cloned.1.call-start = ((), (), s32[]{:S(2)}) async-start(), calls=%async_computation.2 | async-start | bytes 12582912 | tf_op jit(solution)/shard_map/reduce_scatter | solution.py:23
  428.7 5.0 copy-start.2
  428.7 5.9 copy-start.3
  428.7 5.9 copy-start.6
  443.3 2.6 copy-start.10
  482.8 70.0 %reduce-scatter.5.cloned.1.call-start = ((), (), s32[]{:S(2)}) async-start(), calls=%async_computation.3 | async-start | bytes 5242880 | tf_op jit(solution)/shard_map/reduce_scatter | solution.py:23
  502.4 120.2 %all-gather.4.cloned.1.call-start = ((), (), s32[]{:S(2)}) async-start(), calls=%async_computation.4 | async-start | bytes 4718592 | tf_op jit(solution)/shard_map/all_gather | solution.py:144
  622.6 7.9 %copy-start.1 = (bf16[512,2048]{1,0:T(8,128)(2,1)S(1)}, bf16[512,2048]{1,0:T(8,128)(2,1)}, u32[]{:S(2)}) copy-start(bf16[512,2048]{1,0:T(8,128)(2,1)} %param.17) | copy-start | bytes 6291460
Sparse Core Ops, SparseCore 0:
  33.5 371.4 all-gather.5
  483.0 19.3 reduce-scatter.2
  504.8 48.0 reduce-scatter.4
  591.1 31.4 all-gather.3
